TPU v7x, 32 devices: a whole 2x2x4 slice. The times are simulated.
32 devices in a mesh: seq: 8 (over z, x), fsdp: 4 (over y, core).
Axes of the slice: x: 2, y: 2, z: 4, core: 2. Of those that a mesh axis runs over, the one named last changes fastest.
Arguments:
- tokens: bfloat16 [4, 1024, 1536], P('fsdp', 'seq'), may hold values from -6 to 6
- in_weight: bfloat16 [1536, 6400], P('fsdp'), may hold values from -0.15625 to 0.15625
- step_weight: bfloat16 [1536, 48], P('fsdp'), may hold values from -0.15625 to 0.15625
- conv_kernel: bfloat16 [4, 3328], P(None, 'fsdp'), may hold values from -3 to 3
- conv_bias: bfloat16 [3328], P('fsdp'), may hold values from -3 to 3
- step_bias: bfloat16 [48], P('fsdp'), may hold values from -6 to -3
- log_decay: bfloat16 [48], P('fsdp'), may hold values from -7 to 1
- skip_gain: bfloat16 [48], P('fsdp'), may hold values from 0.5 to 1.5
- gate_gain: bfloat16 [3072], P('fsdp'), may hold values from 0.5 to 1.5
- norm_gain: bfloat16 [1536], P('fsdp'), may hold values from 0.5 to 1.5
- out_weight: bfloat16 [3072, 1536], P('fsdp'), may hold values from -0.109375 to 0.109375
- cotangent: bfloat16 [4, 1024, 1536], P('fsdp', 'seq'), may hold values from -6 to 6
Outputs:
- block_out: bfloat16 [4, 1024, 1536], P('fsdp', 'seq')
- input_grad: float32 [4, 1024, 1536], P('fsdp', 'seq')
- in_weight_grad: float32 [1536, 6400], P('fsdp')
- step_weight_grad: float32 [1536, 48], P('fsdp')
- conv_kernel_grad: float32 [4, 3328], P(None, 'fsdp')
- conv_bias_grad: float32 [3328], P('fsdp')
- step_bias_grad: float32 [48], P('fsdp')
- log_decay_grad: float32 [48], P('fsdp')
- skip_gain_grad: float32 [48], P('fsdp')
- gate_gain_grad: float32 [3072], P('fsdp')
- norm_gain_grad: float32 [1536], P('fsdp')
- out_weight_grad: float32 [3072, 1536], P('fsdp')
All inputs are finite; a program needn't handle non-finite values.
Results may differ from a plain program's by a relative error of at most 0.012.
The roundings to bfloat16 on the way count: a program that leaves them out, or rounds other values in their place, can miss the bound.
Values may be sent and summed in bfloat16 or wider, within the bound.
A program may use at most 320 MiB of HBM per device.

v0:
```python
import jax
import jax.numpy as jnp
from jax import lax
from jax.sharding import PartitionSpec as P

N = 128
BLOCK = 256
epsilon = 1e-05
highest = lax.Precision.HIGHEST


def block_step(carried, pieces, decay_rate):
    x_blk, step_blk, b_blk, c_blk = pieces
    cumulative = jnp.cumsum(step_blk * decay_rate[None, :], axis=0).T
    positions = jnp.arange(step_blk.shape[0])
    triangle = positions[:, None] >= positions[None, :]
    log_gap = jnp.where(triangle[None], cumulative[:, :, None] - cumulative[:, None, :], -1e30)
    scores = jnp.dot(c_blk, b_blk.T, precision=highest)
    mixing = jnp.exp(log_gap) * scores[None] * step_blk.T[:, None, :]
    y_inside = jnp.einsum("hij,jhp->ihp", mixing, x_blk, precision=highest)
    y_carried = jnp.exp(cumulative).T[:, :, None] * jnp.einsum(
        "in,hpn->ihp", c_blk, carried, precision=highest
    )
    weighting = jnp.exp(cumulative[:, -1:] - cumulative) * step_blk.T
    renewed = jnp.exp(cumulative[:, -1])[:, None, None] * carried + jnp.einsum(
        "hj,jhp,jn->hpn", weighting, x_blk, b_blk, precision=highest
    )
    return (renewed, y_inside + y_carried)


def ssd_scan(x_heads, step_size, decay_rate, b_conv, c_conv, carried):
    length = step_size.shape[0]
    extent = min(BLOCK, length)
    number = length // extent
    pieces = (
        x_heads.reshape((number, extent) + x_heads.shape[1:]),
        step_size.reshape((number, extent) + step_size.shape[1:]),
        b_conv.reshape(number, extent, -1),
        c_conv.reshape(number, extent, -1),
    )

    def advance(ssm_state, block_in):
        return block_step(ssm_state, block_in, decay_rate)

    finals, outputs = lax.scan(jax.checkpoint(advance), carried, pieces)
    return outputs.reshape(x_heads.shape)


def prepare(extended, raw_steps, conv_kernel, conv_offset, step_bias, log_rates):
    kernel_width = conv_kernel.shape[0]
    length = extended.shape[0] - kernel_width + 1
    summed = conv_offset[None, :] + sum(
        (
            conv_kernel[offset][None, :] * extended[offset : offset + length]
            for offset in range(kernel_width)
        )
    )
    active = jax.nn.silu(summed)
    split_at = active.shape[1] - 2 * N
    step_size = jax.nn.softplus(raw_steps + step_bias[None, :])
    return (
        active[:, :split_at],
        active[:, split_at : split_at + N],
        active[:, split_at + N :],
        step_size,
        -jnp.exp(log_rates),
    )


def mix_out(x_conv, b_conv, c_conv, step_size, decay_rate, gate_in, skip_part, carried):
    length, head_count = step_size.shape
    x_heads = x_conv.reshape(length, head_count, -1)
    result = (
        ssd_scan(x_heads, step_size, decay_rate, b_conv, c_conv, carried)
        + skip_part[None, :, None] * x_heads
    )
    return result.reshape(length, -1) * jax.nn.silu(gate_in)


def rms_forward(values, gains):
    scaling = lax.rsqrt(jnp.mean(values * values, axis=-1, keepdims=True) + epsilon)
    return (values * scaling * gains[None, :], scaling)


def rms_backward(values, gains, scaling, upstream):
    weighted = upstream * gains[None, :]
    gain_grad = jnp.sum(upstream * values * scaling, axis=0)
    inner_mean = jnp.mean(weighted * values, axis=-1, keepdims=True)
    return (scaling * weighted - scaling**3 * values * inner_mean, gain_grad)


def contract(left, right, left_dim, right_dim):
    return lax.dot_general(
        left, right, (((left_dim,), (right_dim,)), ((), ())), preferred_element_type=jnp.float32
    )


def reorder(gradient, axis_pos, outer_count, inner_count):
    moved_axis = jnp.moveaxis(gradient, axis_pos, 0)
    regrouped = moved_axis.reshape((outer_count, inner_count, -1) + moved_axis.shape[1:])
    swapped = jnp.swapaxes(regrouped, 0, 1).reshape(moved_axis.shape)
    return jnp.moveaxis(swapped, 0, axis_pos)


def place_slice(part, total_len, start_at, axis_pos):
    zeros_shape = part.shape[:axis_pos] + (total_len,) + part.shape[axis_pos + 1 :]
    anchor = tuple((start_at if index_pos == axis_pos else 0 for index_pos in range(part.ndim)))
    return lax.dynamic_update_slice(jnp.zeros(zeros_shape, jnp.float32), part, anchor)


def shards(
    tokens,
    in_weight,
    step_weight,
    conv_kernel,
    conv_bias,
    step_bias,
    log_decay,
    skip_gain,
    gate_gain,
    norm_gain,
    out_weight,
    cotangent,
):
    gathered = (
        lax.all_gather(in_weight, "fsdp", axis=0, tiled=True),
        lax.all_gather(step_weight, "fsdp", axis=0, tiled=True),
        lax.all_gather(conv_kernel, "fsdp", axis=1, tiled=True),
        lax.all_gather(conv_bias, "fsdp", axis=0, tiled=True),
        lax.all_gather(step_bias, "fsdp", axis=0, tiled=True),
        lax.all_gather(log_decay, "fsdp", axis=0, tiled=True),
        lax.all_gather(skip_gain, "fsdp", axis=0, tiled=True),
        lax.all_gather(gate_gain, "fsdp", axis=0, tiled=True),
        lax.all_gather(norm_gain, "fsdp", axis=0, tiled=True),
        lax.all_gather(out_weight, "fsdp", axis=0, tiled=True),
    )
    w_in = gathered[0]
    w_step = gathered[1]
    w_out = gathered[9]
    kernel_f = gathered[2].astype(jnp.float32)
    bias_f = gathered[3].astype(jnp.float32)
    step_bias_f = gathered[4].astype(jnp.float32)
    decay_f = gathered[5].astype(jnp.float32)
    skip_f = gathered[6].astype(jnp.float32)
    gate_f = gathered[7].astype(jnp.float32)
    norm_f = gathered[8].astype(jnp.float32)
    inner_width = w_out.shape[0]
    head_count = w_step.shape[1]
    head_size = inner_width // head_count
    kernel_width = kernel_f.shape[0]
    out_cotangent = cotangent[0]
    residual = tokens[0].astype(jnp.float32)
    normed, scale_in = rms_forward(residual, norm_f)
    hidden = normed.astype(jnp.bfloat16)
    projected = jnp.dot(hidden, w_in, preferred_element_type=jnp.float32).astype(jnp.bfloat16)
    raw_steps = jnp.dot(hidden, w_step, preferred_element_type=jnp.float32).astype(jnp.bfloat16)
    seq_count = lax.axis_size("seq")
    position = lax.axis_index("seq")
    head_group = head_count // seq_count
    columns = head_group * head_size
    col_start = position * columns
    head_start = position * head_group
    tiled_bc = jnp.tile(projected[:, 2 * inner_width :], (1, seq_count))
    gate_part, x_part, step_part, bc_part = (
        lax.all_to_all(projected[:, :inner_width], "seq", split_axis=1, concat_axis=0, tiled=True),
        lax.all_to_all(
            projected[:, inner_width : 2 * inner_width],
            "seq",
            split_axis=1,
            concat_axis=0,
            tiled=True,
        ),
        lax.all_to_all(raw_steps, "seq", split_axis=1, concat_axis=0, tiled=True),
        lax.all_to_all(tiled_bc, "seq", split_axis=1, concat_axis=0, tiled=True),
    )
    my_kernel = jnp.concatenate(
        [lax.dynamic_slice_in_dim(kernel_f, col_start, columns, 1), kernel_f[:, inner_width:]],
        axis=1,
    )
    my_bias = jnp.concatenate(
        [lax.dynamic_slice_in_dim(bias_f, col_start, columns, 0), bias_f[inner_width:]], axis=0
    )
    my_step_bias = lax.dynamic_slice_in_dim(step_bias_f, head_start, head_group, 0)
    my_decay = lax.dynamic_slice_in_dim(decay_f, head_start, head_group, 0)
    my_skip = lax.dynamic_slice_in_dim(skip_f, head_start, head_group, 0)
    padding = jnp.zeros((kernel_width - 1, columns + 2 * N), jnp.float32)
    extended = jnp.concatenate(
        [padding, jnp.concatenate([x_part, bc_part], axis=1).astype(jnp.float32)], axis=0
    )
    prepared, pull_prepare = jax.vjp(
        prepare, extended, step_part.astype(jnp.float32), my_kernel, my_bias, my_step_bias, my_decay
    )
    x_conv, b_conv, c_conv, step_size, decay_rate = prepared
    start_state = jnp.zeros((head_group, head_size, N), jnp.float32)
    gated_f, pull_mix = jax.vjp(
        mix_out,
        x_conv,
        b_conv,
        c_conv,
        step_size,
        decay_rate,
        gate_part.astype(jnp.float32),
        my_skip,
        start_state,
    )
    gated_out = lax.all_to_all(
        gated_f.astype(jnp.bfloat16), "seq", split_axis=0, concat_axis=1, tiled=True
    )
    gated_back = gated_out.astype(jnp.float32)
    mixed_f, scale_out = rms_forward(gated_back, gate_f)
    mixed_norm = mixed_f.astype(jnp.bfloat16)
    block_out = (residual + jnp.dot(mixed_norm, w_out, preferred_element_type=jnp.float32)).astype(
        jnp.bfloat16
    )
    out_grad = contract(mixed_norm, out_cotangent, 0, 0)
    mixed_grad = contract(out_cotangent, w_out, 1, 1)
    gated_grad, gate_gain_grad = rms_backward(gated_back, gate_f, scale_out, mixed_grad)
    gated_grad_b = lax.optimization_barrier(gated_grad.astype(jnp.bfloat16))
    gated_grad_h = lax.all_to_all(
        gated_grad_b, "seq", split_axis=1, concat_axis=0, tiled=True
    ).astype(jnp.float32)
    x_grad, b_grad, c_grad, step_grad, rate_grad, gate_in_grad, skip_grad_h, unused = pull_mix(
        gated_grad_h
    )
    ext_grad, raw_grad, kernel_grad_h, bias_grad_h, step_bias_grad_h, decay_grad_h = pull_prepare(
        (x_grad, b_grad, c_grad, step_grad, rate_grad)
    )
    body_grad = ext_grad[kernel_width - 1 :]
    gate_back, x_back, step_back = (
        lax.all_to_all(
            gate_in_grad.astype(jnp.bfloat16), "seq", split_axis=0, concat_axis=1, tiled=True
        ),
        lax.all_to_all(
            body_grad[:, :columns].astype(jnp.bfloat16),
            "seq",
            split_axis=0,
            concat_axis=1,
            tiled=True,
        ),
        lax.all_to_all(
            raw_grad.astype(jnp.bfloat16), "seq", split_axis=0, concat_axis=1, tiled=True
        ),
    )
    bc_back = lax.psum_scatter(
        body_grad[:, columns:].astype(jnp.bfloat16), "seq", scatter_dimension=0, tiled=True
    )
    proj_grad = jnp.concatenate([gate_back, x_back, bc_back], axis=1)
    kernel_grad = jnp.concatenate(
        [
            place_slice(kernel_grad_h[:, :columns], inner_width, col_start, 1),
            kernel_grad_h[:, columns:],
        ],
        axis=1,
    )
    bias_grad = jnp.concatenate(
        [place_slice(bias_grad_h[:columns], inner_width, col_start, 0), bias_grad_h[columns:]],
        axis=0,
    )
    step_bias_grad = place_slice(step_bias_grad_h, head_count, head_start, 0)
    decay_grad = place_slice(decay_grad_h, head_count, head_start, 0)
    skip_grad = place_slice(skip_grad_h, head_count, head_start, 0)
    in_grad = contract(hidden, proj_grad, 0, 0)
    step_w_grad = contract(hidden, step_back, 0, 0)
    hidden_grad = contract(proj_grad, w_in, 1, 1) + contract(step_back, w_step, 1, 1)
    resid_grad, norm_gain_grad = rms_backward(residual, norm_f, scale_in, hidden_grad)
    input_grad = out_cotangent.astype(jnp.float32) + resid_grad
    fsdp_count = lax.axis_size("fsdp")
    seq_total = lax.axis_size("seq")

    def spread_heads(gradient):
        return jnp.tile(gradient.reshape(fsdp_count, -1), (seq_total, 1)).reshape(-1)

    blocks = (
        lax.psum_scatter(
            reorder(in_grad, 0, fsdp_count, seq_total),
            ("seq", "fsdp"),
            scatter_dimension=0,
            tiled=True,
        ),
        lax.psum_scatter(
            reorder(step_w_grad, 0, fsdp_count, seq_total),
            ("seq", "fsdp"),
            scatter_dimension=0,
            tiled=True,
        ),
        lax.psum_scatter(
            reorder(kernel_grad, 1, fsdp_count, seq_total),
            ("seq", "fsdp"),
            scatter_dimension=1,
            tiled=True,
        ),
        lax.psum_scatter(
            reorder(bias_grad, 0, fsdp_count, seq_total),
            ("seq", "fsdp"),
            scatter_dimension=0,
            tiled=True,
        ),
        lax.psum_scatter(
            spread_heads(step_bias_grad), ("seq", "fsdp"), scatter_dimension=0, tiled=True
        ),
        lax.psum_scatter(
            spread_heads(decay_grad), ("seq", "fsdp"), scatter_dimension=0, tiled=True
        ),
        lax.psum_scatter(spread_heads(skip_grad), ("seq", "fsdp"), scatter_dimension=0, tiled=True),
        lax.psum_scatter(
            reorder(gate_gain_grad, 0, fsdp_count, seq_total),
            ("seq", "fsdp"),
            scatter_dimension=0,
            tiled=True,
        ),
        lax.psum_scatter(
            reorder(norm_gain_grad, 0, fsdp_count, seq_total),
            ("seq", "fsdp"),
            scatter_dimension=0,
            tiled=True,
        ),
        lax.psum_scatter(
            reorder(out_grad, 0, fsdp_count, seq_total),
            ("seq", "fsdp"),
            scatter_dimension=0,
            tiled=True,
        ),
    )
    joined = (
        lax.all_gather(blocks[0], "seq", axis=0, tiled=True),
        lax.all_gather(blocks[1], "seq", axis=0, tiled=True),
        lax.all_gather(blocks[2], "seq", axis=1, tiled=True),
        lax.all_gather(blocks[3], "seq", axis=0, tiled=True),
        lax.all_gather(blocks[7], "seq", axis=0, tiled=True),
        lax.all_gather(blocks[8], "seq", axis=0, tiled=True),
        lax.all_gather(blocks[9], "seq", axis=0, tiled=True),
    )
    totals = (
        joined[0],
        joined[1],
        joined[2],
        joined[3],
        blocks[4],
        blocks[5],
        blocks[6],
        joined[4],
        joined[5],
        joined[6],
    )
    return (
        block_out[None],
        input_grad[None],
        totals[0],
        totals[1],
        totals[2],
        totals[3],
        totals[4],
        totals[5],
        totals[6],
        totals[7],
        totals[8],
        totals[9],
    )


def solution(mesh):
    placed = (
        P("fsdp", "seq", None),
        P("fsdp", None),
        P("fsdp", None),
        P(None, "fsdp"),
        P("fsdp"),
        P("fsdp"),
        P("fsdp"),
        P("fsdp"),
        P("fsdp"),
        P("fsdp"),
        P("fsdp", None),
        P("fsdp", "seq", None),
    )
    return jax.shard_map(
        shards,
        mesh=mesh,
        in_specs=placed,
        out_specs=(
            P("fsdp", "seq", None),
            P("fsdp", "seq", None),
            P("fsdp", None),
            P("fsdp", None),
            P(None, "fsdp"),
            P("fsdp"),
            P("fsdp"),
            P("fsdp"),
            P("fsdp"),
            P("fsdp"),
            P("fsdp"),
            P("fsdp", None),
        ),
        check_vma=False,
    )
```

profile of v0, /device:TPU:0, one launch (start us, length us, event | category | flops | bytes accessed | tf_op | source)
XLA Modules:
  0.0 1683.6 jit_solution(14580512450812876870)
XLA Ops:
  28.3 108.3 %all-gather.9.cloned.1.call-done = bf16[1536,6400]{1,0:T(8,128)(2,1)} async-done(((bf16[384,6400]{1,0:T(8,128)(2,1)}), bf16[1536,6400]{1,0:T(8,128)(2,1)}) %all-gather.9.cloned.1.call-update) | async-done | bytes 19660816 | tf_op jit(solution)/shard_map/all_gather | solution.py:126
  154.5 12.8 all-to-all-done.2
  211.3 74.2 %while.41 = (s32[]{:T(128)}, f32[6,64,128]{2,1,0:T(8,128)S(1)}, f32[4,256,6,64]{1,0,3,2:T(4,128)}, f32[4,6,64,128]{3,2,1,0:T(8,128)}, f32[4,256,6]{1,2,0:T(8,128...) while((s32[]{:T(128)}, f32[6,64,128]{2,1,0:T(8,128)S(1)}, ...), condition=%wide.region_4.5_spmd.clone, body=%wide.region_1.4_spmd.clone.sunk | while | flops 706957824 | bytes 5773208 | solution.py:45
  310.4 14.1 all-to-all-done.4
  346.8 14.6 all-to-all-done.5
  376.5 167.4 %while.42 = (s32[]{:T(128)}, f32[6]{0:T(128)}, f32[6,64,128]{2,1,0:T(8,128)S(1)}, f32[4,256,6,64]{1,0,3,2:T(4,128)}, f32[4,256,6]{1,2,0:T(8,128)}, /*index=5*/f3...) while((s32[]{:T(128)}, f32[6]{0:T(128)}, ...), condition=%wide.region_20.21_spmd.clone, body=%wide.region_7.20_spmd.clone.sunk | while | flops 1669247488 | bytes 18030544 | solution.py:45
  402.7 9.5 dynamic_update_slice.93
  444.6 9.5 dynamic_update_slice.93
  528.3 9.5 dynamic_update_slice.93
  575.7 9.9 all_to_all.141
  595.2 13.1 all-to-all-done.6
  613.6 21.0 %all-to-all-done.7 = bf16[8,128,384]{2,1,0:T(8,128)(2,1)} async-done(((bf16[8,128,384]{2,1,0:T(8,128)(2,1)}), bf16[8,128,384]{2,1,0:T(8,128)(2,1)}, u32[]{:S(2)}, u32[]{:S(2)}) %all-to-all-start.7) | async-done | bytes 786464 | tf_op jit(solution)/shard_map/all_to_all | solution.py:233
  639.3 12.3 fusion.152
  653.8 20.1 %convolution_bitcast_fusion.2 = f32[8,4,48,6400]{3,2,0,1:T(8,128)} fusion(bf16[4,8,48,128]{3,2,1,0:T(8,128)(2,1)S(1)} %bitcast.577, bf16[128,6400]{1,0:T(8,128)(2,1)} %constant_dynamic-update-slice_fusion), kind=kOutput, calls=%fused_computation.128 | convolution fusion | flops 2516582400 | bytes 41353216 | tf_op jit(solution)/shard_map/dot_general | solution.py:93
  673.9 28.6 %copy.323 = f32[8,4,48,6400]{3,2,1,0:T(8,128)} copy(f32[8,4,48,6400]{3,2,0,1:T(8,128)} %convolution_bitcast_fusion.2) | data formatting | bytes 78643200 | tf_op jit(solution)/shard_map/transpose | solution.py:101
  711.7 130.3 %reduce-scatter.12.cloned.1.call-done = f32[96,1536]{1,0:T(8,128)} async-done(((f32[3072,1536]{1,0:T(8,128)}), f32[96,1536]{1,0:T(8,128)}) %reduce-scatter.12.cloned.1.call-update) | async-done | bytes 589840 | tf_op jit(solution)/shard_map/reduce_scatter | solution.py:317
  842.1 364.2 %reduce-scatter.10.cloned.1.call-done = f32[48,6400]{1,0:T(8,128)} async-done(((f32[1536,6400]{1,0:T(8,128)}), f32[48,6400]{1,0:T(8,128)}) %reduce-scatter.10.cloned.1.call-update) | async-done | bytes 1228816 | tf_op jit(solution)/shard_map/reduce_scatter | solution.py:274
  1214.8 123.9 %all-reduce.33.cloned.1.call-done = (f32[4,3328]{1,0:T(4,128)}, f32[3328]{0:T(1024)}, f32[384]{0:T(512)}, f32[384]{0:T(512)}, f32[384]{0:T(512)}, /*index=5*/f32[3072]{0:T(1024)}, f32[1536]{0:T(1024)}) async-done(((f32[4,3328]{1,0:T(4,128)}, f32[3328]{0:T(1024)}, f32[384]{0:T(512)}, f32[384]{0:T(512)}, f32[384]{0:T(512)}, /*index=5*/f32[3072]{0:T(1024)}, f32[1536]{0:T(1024)}), (f32[4,3328]{1,0:T(4,128)}, ...) | async-done | bytes 89616
  1339.5 27.0 %all-gather.3 = f32[8,104,4]{1,2,0:T(4,128)S(1)} all-gather(f32[1,104,4]{1,2,0:T(4,128)S(1)} %dynamic-slice_bitcast_fusion.7), channel_id=1, replica_groups=mesh['seq'=8,'fsdp'=4] {'seq'}, dimensions={0}, use_global_device_ids=true | all-gather | bytes 14976 | tf_op jit(solution)/shard_map/all_gather | solution.py:327
  1373.5 35.5 %all-reduce.29 = (f32[832]{0:T(1024)}, f32[768]{0:T(1024)}, f32[384]{0:T(512)}) all-reduce(f32[832]{0:T(1024)S(1)} %dynamic-slice_dynamic-update-slice_fusion.2, f32[768]{0:T(1024)S(1)} %dynamic-slice_dynamic-update-slice_fusion.1, f32[384]{0:T(512)S(1)} %dynamic-slice_dynamic-update-slice_fusion), channel_id=1, replica_groups=mesh['seq'=8,'fsdp'=4] {'seq'}, use_global_device_ids=true, to_apply=%add.18 | all-reduce | flops 1984 | bytes 15872
  1409.1 32.7 %reduce-scatter.14.cloned.1.call-done = f32[48,48]{1,0:T(8,128)} async-done(((f32[1536,48]{1,0:T(8,128)}), f32[48,48]{1,0:T(8,128)}) %reduce-scatter.14.cloned.1.call-update) | async-done | bytes 9232 | tf_op jit(solution)/shard_map/reduce_scatter | solution.py:280
  1441.8 32.1 %all_gather.62 = f32[384,48]{1,0:T(8,128)S(1)} all-gather(f32[48,48]{1,0:T(8,128)} %reduce-scatter.14.cloned.1.call-done), channel_id=1, replica_groups=mesh['seq'=8,'fsdp'=4] {'seq'}, dimensions={0}, use_global_device_ids=true | all-gather | bytes 82944 | tf_op jit(solution)/shard_map/all_gather | solution.py:326
  1474.6 48.8 %all-gather.15.cloned.1.call-done = f32[768,1536]{1,0:T(8,128)} async-done(((f32[96,1536]{1,0:T(8,128)}), f32[768,1536]{1,0:T(8,128)}) %all-gather.15.cloned.1.call-update) | async-done | bytes 4718608 | tf_op jit(solution)/shard_map/all_gather | solution.py:331
  1523.4 142.8 %all-gather.13.cloned.1.call-done = f32[384,6400]{1,0:T(8,128)} async-done(((f32[48,6400]{1,0:T(8,128)}), f32[384,6400]{1,0:T(8,128)}) %all-gather.13.cloned.1.call-update) | async-done | bytes 9830416 | tf_op jit(solution)/shard_map/all_gather | solution.py:325
  (656 shorter events, 442.9 us)
Async XLA Ops:
  7.2 129.5 %all-gather.9.cloned.1.call-start = ((), (), s32[]{:S(2)}) async-start(), calls=%async_computation.13 | async-start | bytes 24576000 | tf_op jit(solution)/shard_map/all_gather | solution.py:126
  14.2 122.5 %copy-start.41 = (f32[1536]{0:T(1024)}, f32[1536]{0:T(1024)S(1)}, u32[]{:S(2)}) copy-start(f32[1536]{0:T(1024)S(1)} %reshape.548) | copy-start | bytes 18436
  20.7 116.0 %copy-start.58 = (f32[128]{0:T(128)}, f32[128]{0:T(128)S(1)}, u32[]{:S(2)}) copy-start(f32[128]{0:T(128)S(1)} %get-tuple-element.798) | copy-start | bytes 1540
  21.6 124.5 %all-to-all-start = ((bf16[128,8,6]{0,2,1:T(8,128)(2,1)}), bf16[128,8,6]{0,2,1:T(8,128)(2,1)S(1)}, u32[]{:S(2)}, u32[]{:S(2)}) async-start(bf16[128,8,6]{0,2,1:T(8,128)(2,1)} %all_to_all.106), calls=%async_computation | async-start | bytes 32768 | tf_op jit(solution)/shard_map/all_to_all | solution.py:173
  27.6 297.5 %all-gather.11.cloned.1.call-start = ((), (), s32[]{:S(2)}) async-start(), calls=%async_computation.14 | async-start | bytes 11796480 | tf_op jit(solution)/shard_map/all_gather | solution.py:135
  146.9 20.4 %all-to-all-start.2 = ((bf16[128,8,256]{2,0,1:T(8,128)(2,1)}), bf16[128,8,256]{2,0,1:T(8,128)(2,1)S(1)}, u32[]{:S(2)}, u32[]{:S(2)}) async-start(bf16[128,8,256]{2,0,1:T(8,128)(2,1)} %tile.28), calls=%async_computation.2 | async-start | bytes 1048576 | tf_op jit(solution)/shard_map/all_to_all | solution.py:174
  167.4 24.0 %all-to-all-start.1 = ((bf16[128,8,384]{2,0,1:T(8,128)(2,1)}), bf16[128,8,384]{2,0,1:T(8,128)(2,1)S(1)}, u32[]{:S(2)}, u32[]{:S(2)}) async-start(bf16[128,8,384]{2,0,1:T(8,128)(2,1)} %bitcast.418), calls=%async_computation.1 | async-start | bytes 1572864 | tf_op jit(solution)/shard_map/all_to_all | solution.py:166
  181.1 160.6 %copy-start.68 = (f32[48]{0:T(128)}, f32[48]{0:T(128)S(1)}, u32[]{:S(2)}) copy-start(f32[48]{0:T(128)S(1)} %convert_element_type.138) | copy-start | bytes 580
  187.1 108.4 %copy-start.55 = (f32[384]{0:T(512)}, f32[384]{0:T(512)S(1)}, u32[]{:S(2)}) copy-start(f32[384]{0:T(512)S(1)} %mul.640) | copy-start | bytes 4612
  191.4 99.3 %all-to-all-start.3 = ((bf16[128,8,384]{0,2,1:T(8,128)(2,1)}), bf16[128,8,384]{0,2,1:T(8,128)(2,1)}, u32[]{:S(2)}, u32[]{:S(2)}) async-start(bf16[128,8,384]{0,2,1:T(8,128)(2,1)} %bitcast.18), calls=%async_computation.3 | async-start | bytes 1572864 | tf_op jit(solution)/shard_map/all_to_all | solution.py:165
  298.9 25.6 %all-to-all-start.4 = ((bf16[8,128,384]{2,1,0:T(8,128)(2,1)}), bf16[8,128,384]{2,1,0:T(8,128)(2,1)S(1)}, u32[]{:S(2)}, u32[]{:S(2)}) async-start(bf16[8,128,384]{2,1,0:T(8,128)(2,1)} %bitcast.580), calls=%async_computation.4 | async-start | bytes 1572864 | tf_op jit(solution)/shard_map/all_to_all | solution.py:206
  337.4 24.1 %all-to-all-start.5 = ((bf16[128,8,384]{0,2,1:T(8,128)(2,1)}), bf16[128,8,384]{0,2,1:T(8,128)(2,1)}, u32[]{:S(2)}, u32[]{:S(2)}) async-start(bf16[128,8,384]{0,2,1:T(8,128)(2,1)} %bitcast.583), calls=%async_computation.5 | async-start | bytes 1572864 | tf_op jit(solution)/shard_map/all_to_all | solution.py:219
  341.6 296.2 %reduce-scatter.8.cloned.1.call-start = ((), (), s32[]{:S(2)}) async-start(), calls=%async_computation.15 | async-start | bytes 589824 | tf_op jit(solution)/shard_map/reduce_scatter | solution.py:244
  563.5 278.5 %reduce-scatter.12.cloned.1.call-start = ((), (), s32[]{:S(2)}) async-start(), calls=%async_computation.18 | async-start | bytes 19464192 | tf_op jit(solution)/shard_map/reduce_scatter | solution.py:317
  585.6 22.7 %all-to-all-start.6 = ((bf16[8,128,384]{2,1,0:T(8,128)(2,1)}), bf16[8,128,384]{2,1,0:T(8,128)(2,1)S(1)}, u32[]{:S(2)}, u32[]{:S(2)}) async-start(bf16[8,128,384]{2,1,0:T(8,128)(2,1)} %bitcast.29), calls=%async_computation.6 | async-start | bytes 1572864 | tf_op jit(solution)/shard_map/all_to_all | solution.py:230
  608.3 26.4 %all-to-all-start.7 = ((bf16[8,128,384]{2,1,0:T(8,128)(2,1)}), bf16[8,128,384]{2,1,0:T(8,128)(2,1)}, u32[]{:S(2)}, u32[]{:S(2)}) async-start(bf16[8,128,384]{2,1,0:T(8,128)(2,1)} %bitcast.584), calls=%async_computation.7 | async-start | bytes 1572864 | tf_op jit(solution)/shard_map/all_to_all | solution.py:233
  612.5 593.8 %reduce-scatter.10.cloned.1.call-start = ((), (), s32[]{:S(2)}) async-start(), calls=%async_computation.16 | async-start | bytes 40550400 | tf_op jit(solution)/shard_map/reduce_scatter | solution.py:274
  702.5 636.2 %all-reduce.33.cloned.1.call-start = ((), (), s32[]{:S(2)}) async-start(), calls=%async_computation.21 | async-start | bytes 192512
  710.4 731.4 %reduce-scatter.14.cloned.1.call-start = ((), (), s32[]{:S(2)}) async-start(), calls=%async_computation.20 | async-start | bytes 811008 | tf_op jit(solution)/shard_map/reduce_scatter | solution.py:280
  711.6 494.7 %copy-start.74 = (u32[32]{0:T(128)S(1)}, u32[32]{0:T(128)}, u32[]{:S(2)}) copy-start(u32[32]{0:T(128)} %constant.200) | copy-start | bytes 388
  711.6 497.3 %copy-start.36 = (f32[4,1,768]{2,1,0:T(1,128)S(1)}, f32[4,1,768]{2,1,0:T(1,128)}, u32[]{:S(2)}) copy-start(f32[4,1,768]{2,1,0:T(1,128)} %copy-done.35) | copy-start | bytes 36868
  711.6 497.3 %copy-start.61 = (f32[128]{0:T(128)S(1)}, f32[128]{0:T(128)}, u32[]{:S(2)}) copy-start(f32[128]{0:T(128)} %copy-done.60) | copy-start | bytes 1540
  711.7 811.7 %all-gather.15.cloned.1.call-start = ((), (), s32[]{:S(2)}) async-start(), calls=%async_computation.19 | async-start | bytes 5308416 | tf_op jit(solution)/shard_map/all_gather | solution.py:331
  842.1 824.1 %all-gather.13.cloned.1.call-start = ((), (), s32[]{:S(2)}) async-start(), calls=%async_computation.17 | async-start | bytes 11059200 | tf_op jit(solution)/shard_map/all_gather | solution.py:325
  (87 other events, 676.3 us)
Sparse Core Ops, SparseCore 0:
  9.6 127.0 all-gather.8
  138.2 64.7 all-gather.10
  563.6 63.3 reduce-scatter.7
  633.3 208.7 reduce-scatter.11
  848.3 357.9 reduce-scatter.9
  1213.8 124.8 all-reduce.32
  1344.4 97.3 reduce-scatter.13
  1444.0 79.3 all-gather.14
  1525.6 140.5 all-gather.12
where the time goes:
time: 1690 us; the launch traced here: 1680 us
  waiting for transfers between devices  1030 us (61%)
  local copies, waits for them, and re-layouts  232 us (14%)
  blocking collectives  135 us (8%)
  matrix products  132 us (8%)
  other arithmetic  96 us (6%)
  starting transfers between devices  38.3 us (2%)
  between operations  18.4 us (1%)
    reduce_scatter x1, waiting for transfers between devices, shards(): lax.psum_scatter(reorder(in_grad, 0, fsdp_count, seq_total), ('seq', 'fsd...  364 us
    all_gather x1, waiting for transfers between devices, shards(): lax.all_gather(blocks[0], 'seq', axis=0, tiled=True)  143 us
    reduce_scatter x1, waiting for transfers between devices, shards(): lax.psum_scatter(reorder(out_grad, 0, fsdp_count, seq_total), ('seq', 'fs...  130 us
    unnamed x10, waiting for transfers between devices  125 us
    all_gather x1, waiting for transfers between devices, shards(): lax.all_gather(in_weight, 'fsdp', axis=0, tiled=True)  108 us
    dynamic_update_slice x16, local copies, waits for them, and re-layouts, ssd_scan(): finals, outputs = lax.scan(jax.checkpoint(advance), carried, pieces)  79.5 us
    another operation x33, other arithmetic  50.7 us
    all_gather x1, waiting for transfers between devices, shards(): lax.all_gather(blocks[9], 'seq', axis=0, tiled=True)  48.8 us
  transfers between devices with their start and end apart: 17, of which 13 were waited for; matrix products, arithmetic and copies ran while one was open for 14% of the time, Pallas kernels for 0%

commit v1 on v0

--- a/solution.py
+++ b/solution.py
@@ -7,6 +7,17 @@
 BLOCK = 256
 epsilon = 1e-05
 highest = lax.Precision.HIGHEST
+
+
+def ring_gather(shard, axis, dim):
+    ways = lax.axis_size(axis)
+    pieces = [shard]
+    for far in range(1, ways):
+        pieces.append(
+            lax.ppermute(pieces[far - 1], axis, [(d, (d - 1) % ways) for d in range(ways)])
+        )
+    line = jnp.concatenate(pieces, axis=dim)
+    return jnp.roll(line, lax.axis_index(axis) * shard.shape[dim], axis=dim)
 
 
 def block_step(carried, pieces, decay_rate):
@@ -123,7 +134,7 @@
     cotangent,
 ):
     gathered = (
-        lax.all_gather(in_weight, "fsdp", axis=0, tiled=True),
+        ring_gather(in_weight, "fsdp", 0),
         lax.all_gather(step_weight, "fsdp", axis=0, tiled=True),
         lax.all_gather(conv_kernel, "fsdp", axis=1, tiled=True),
         lax.all_gather(conv_bias, "fsdp", axis=0, tiled=True),

time: 1690 us -> 1800 us (1.065)
  blocking collectives: 135 us -> 198 us
  local copies, waits for them, and re-layouts: 232 us -> 272 us
  waiting for transfers between devices: 1030 us -> 1010 us
    all_gather x1 -> x0, waiting for transfers between devices: 108 us -> none  [shards(): lax.all_gather(in_weight, 'fsdp', axis=0, tiled=True)]
    ppermute x0 -> x3, waiting for transfers between devices: none -> 108 us  [ring_gather(): lax.ppermute(pieces[far - 1], axis, [(d, (d - 1) % ways) for d in range(w...]
    all_gather x1, blocking collectives: 6.18 us -> 55.3 us  [shards(): lax.all_gather(norm_gain, 'fsdp', axis=0, tiled=True)]
    unnamed x173 -> x198, local copies, waits for them, and re-layouts: 41.2 us -> 74.2 us
    all_to_all x1, waiting for transfers between devices: 21 us -> 1.41 us  [shards(): lax.all_to_all(raw_grad.astype(jnp.bfloat16), 'seq', split_axis=0, concat...]
    unnamed x10 -> x9, waiting for transfers between devices: 125 us -> 125 us
  transfers between devices with their start and end apart: 17 -> 19, of which waited for: 13 -> 14; matrix products, arithmetic and copies ran while one was open for 14% -> 15% of each run, Pallas kernels for 0% -> 0%
where the time goes in v1:
time: 1800 us; the launch traced here: 1780 us
  waiting for transfers between devices  1010 us (56%)
  local copies, waits for them, and re-layouts  272 us (15%)
  blocking collectives  198 us (11%)
  matrix products  132 us (7%)
  other arithmetic  105 us (6%)
  starting transfers between devices  43.4 us (2%)
  between operations  19 us (1%)
    reduce_scatter x1, waiting for transfers between devices, shards(): lax.psum_scatter(reorder(in_grad, 0, fsdp_count, seq_total), ('seq', 'fsd...  364 us
    all_gather x1, waiting for transfers between devices, shards(): lax.all_gather(blocks[0], 'seq', axis=0, tiled=True)  143 us
    reduce_scatter x1, waiting for transfers between devices, shards(): lax.psum_scatter(reorder(out_grad, 0, fsdp_count, seq_total), ('seq', 'fs...  129 us
    unnamed x9, waiting for transfers between devices  125 us
    ppermute x3, waiting for transfers between devices, ring_gather(): lax.ppermute(pieces[far - 1], axis, [(d, (d - 1) % ways) for d in range(w...  108 us
    dynamic_update_slice x16, local copies, waits for them, and re-layouts, ssd_scan(): finals, outputs = lax.scan(jax.checkpoint(advance), carried, pieces)  79.4 us
    unnamed x198, local copies, waits for them, and re-layouts  74.2 us
    all_gather x1, blocking collectives, shards(): lax.all_gather(norm_gain, 'fsdp', axis=0, tiled=True)  55.3 us
  transfers between devices with their start and end apart: 19, of which 14 were waited for; matrix products, arithmetic and copies ran while one was open for 15% of the time, Pallas kernels for 0%

profile of v1, /device:TPU:0, one launch (start us, length us, event | category | flops | bytes accessed | tf_op | source)
XLA Modules:
  0.0 1783.3 jit_solution(2049201620524090755)
XLA Ops:
  9.7 54.1 %collective-permute-done = bf16[384,6400]{1,0:T(8,128)(2,1)S(1)} collective-permute-done((bf16[384,6400]{1,0:T(8,128)(2,1)}, bf16[384,6400]{1,0:T(8,128)(2,1)S(1)}, u32[]{:S(2)}, u32[]{:S(2)}) %collective-permute-start) | collective-permute-done | bytes 4915232 | tf_op jit(solution)/shard_map/ppermute | solution.py:17
  67.8 53.7 %collective-permute-done.1 = bf16[384,6400]{1,0:T(8,128)(2,1)} collective-permute-done((bf16[384,6400]{1,0:T(8,128)(2,1)S(1)}, bf16[384,6400]{1,0:T(8,128)(2,1)}, u32[]{:S(2)}, u32[]{:S(2)}) %collective-permute-start.1) | collective-permute-done | bytes 4915232 | tf_op jit(solution)/shard_map/ppermute | solution.py:17
  124.2 55.3 %all-gather = bf16[4,1,384]{2,1,0:T(2,128)(2,1)S(1)} all-gather(bf16[1,1,384]{2,1,0:T(2,128)(2,1)S(1)} %reshape.540), channel_id=1, replica_groups=mesh['seq'=8,'fsdp'=4] {'fsdp'}, dimensions={0}, use_global_device_ids=true | all-gather | bytes 3840 | tf_op jit(solution)/shard_map/all_gather | solution.py:145
  230.1 12.8 fusion.97
  253.4 12.1 all-to-all-done.2
  308.6 74.3 %while.41 = (s32[]{:T(128)}, f32[6,64,128]{2,1,0:T(8,128)S(1)}, f32[4,256,6,64]{1,0,3,2:T(4,128)}, f32[4,6,64,128]{3,2,1,0:T(8,128)}, f32[4,256,6]{1,2,0:T(8,128...) while((s32[]{:T(128)}, f32[6,64,128]{2,1,0:T(8,128)S(1)}, ...), condition=%wide.region_4.5_spmd.clone, body=%wide.region_1.4_spmd.clone.sunk | while | flops 706957824 | bytes 5773705 | solution.py:56
  315.4 9.5 dynamic_update_slice.89
  407.9 13.6 all-to-all-done.4
  444.2 14.1 all-to-all-done.5
  473.3 169.8 %while.42 = (s32[]{:T(128)}, f32[6]{0:T(128)}, f32[6,64,128]{2,1,0:T(8,128)S(1)}, f32[4,256,6,64]{1,0,3,2:T(4,128)}, f32[4,256,6]{1,2,0:T(8,128)}, /*index=5*/f3...) while((s32[]{:T(128)}, f32[6]{0:T(128)}, ...), condition=%wide.region_20.21_spmd.clone, body=%wide.region_7.20_spmd.clone.sunk | while | flops 1669247488 | bytes 16049488 | solution.py:56
  685.9 24.3 %all_to_all.141 = bf16[8,128,384]{2,1,0:T(8,128)(2,1)S(1)} all-to-all(bf16[8,128,384]{2,1,0:T(8,128)(2,1)S(1)} %bitcast.588), channel_id=1, replica_groups=mesh['seq'=8,'fsdp'=4] {'seq'}, dimensions={0} | all-to-all | bytes 1572864 | tf_op jit(solution)/shard_map/all_to_all | solution.py:244
  716.0 19.5 %all-to-all-done.6 = bf16[8,128,384]{2,1,0:T(8,128)(2,1)S(1)} async-done(((bf16[8,128,384]{2,1,0:T(8,128)(2,1)}), bf16[8,128,384]{2,1,0:T(8,128)(2,1)S(1)}, u32[]{:S(2)}, u32[]{:S(2)}) %all-to-all-start.6) | async-done | bytes 786464 | tf_op jit(solution)/shard_map/all_to_all | solution.py:241
  737.7 14.0 fusion.126
  755.2 19.5 %convolution_bitcast_fusion.2 = f32[8,4,48,6400]{3,2,0,1:T(8,128)} fusion(bf16[4,8,48,128]{3,2,1,0:T(8,128)(2,1)} %bitcast.579, bf16[128,6400]{1,0:T(8,128)(2,1)S(1)} %constant_dynamic-update-slice_fusion.8), kind=kOutput, calls=%fused_computation.128 | convolution fusion | flops 2516582400 | bytes 41353216 | tf_op jit(solution)/shard_map/dot_general | solution.py:104
  774.7 28.4 %copy.323 = f32[8,4,48,6400]{3,2,1,0:T(8,128)} copy(f32[8,4,48,6400]{3,2,0,1:T(8,128)} %convolution_bitcast_fusion.2) | data formatting | bytes 78643200 | tf_op jit(solution)/shard_map/transpose | solution.py:112
  812.4 129.1 %reduce-scatter.12.cloned.1.call-done = f32[96,1536]{1,0:T(8,128)} async-done(((f32[3072,1536]{1,0:T(8,128)}), f32[96,1536]{1,0:T(8,128)}) %reduce-scatter.12.cloned.1.call-update) | async-done | bytes 589840 | tf_op jit(solution)/shard_map/reduce_scatter | solution.py:328
  941.5 364.1 %reduce-scatter.10.cloned.1.call-done = f32[48,6400]{1,0:T(8,128)} async-done(((f32[1536,6400]{1,0:T(8,128)}), f32[48,6400]{1,0:T(8,128)}) %reduce-scatter.10.cloned.1.call-update) | async-done | bytes 1228816 | tf_op jit(solution)/shard_map/reduce_scatter | solution.py:285
  1314.2 123.8 %all-reduce.33.cloned.1.call-done = (f32[4,3328]{1,0:T(4,128)}, f32[3328]{0:T(1024)}, f32[384]{0:T(512)}, f32[384]{0:T(512)}, f32[384]{0:T(512)}, /*index=5*/f32[3072]{0:T(1024)}, f32[1536]{0:T(1024)}) async-done(((f32[4,3328]{1,0:T(4,128)}, f32[3328]{0:T(1024)}, f32[384]{0:T(512)}, f32[384]{0:T(512)}, f32[384]{0:T(512)}, /*index=5*/f32[3072]{0:T(1024)}, f32[1536]{0:T(1024)}), (f32[4,3328]{1,0:T(4,128)}, ...) | async-done | bytes 89616
  1438.8 27.0 %all-gather.3 = f32[8,104,4]{1,2,0:T(4,128)S(1)} all-gather(f32[1,104,4]{1,2,0:T(4,128)S(1)} %dynamic-slice_bitcast_fusion.7), channel_id=1, replica_groups=mesh['seq'=8,'fsdp'=4] {'seq'}, dimensions={0}, use_global_device_ids=true | all-gather | bytes 14976 | tf_op jit(solution)/shard_map/all_gather | solution.py:338
  1472.8 35.5 %all-reduce.29 = (f32[832]{0:T(1024)}, f32[768]{0:T(1024)}, f32[384]{0:T(512)}) all-reduce(f32[832]{0:T(1024)S(1)} %dynamic-slice_dynamic-update-slice_fusion.2, f32[768]{0:T(1024)S(1)} %dynamic-slice_dynamic-update-slice_fusion.1, f32[384]{0:T(512)S(1)} %dynamic-slice_dynamic-update-slice_fusion), channel_id=1, replica_groups=mesh['seq'=8,'fsdp'=4] {'seq'}, use_global_device_ids=true, to_apply=%add.18 | all-reduce | flops 1984 | bytes 15872
  1508.3 32.6 %reduce-scatter.14.cloned.1.call-done = f32[48,48]{1,0:T(8,128)} async-done(((f32[1536,48]{1,0:T(8,128)}), f32[48,48]{1,0:T(8,128)}) %reduce-scatter.14.cloned.1.call-update) | async-done | bytes 9232 | tf_op jit(solution)/shard_map/reduce_scatter | solution.py:291
  1541.0 32.1 %all_gather.58 = f32[384,48]{1,0:T(8,128)S(1)} all-gather(f32[48,48]{1,0:T(8,128)} %reduce-scatter.14.cloned.1.call-done), channel_id=1, replica_groups=mesh['seq'=8,'fsdp'=4] {'seq'}, dimensions={0}, use_global_device_ids=true | all-gather | bytes 82944 | tf_op jit(solution)/shard_map/all_gather | solution.py:337
  1573.8 48.8 %all-gather.12.cloned.1.call-done = f32[768,1536]{1,0:T(8,128)} async-done(((f32[96,1536]{1,0:T(8,128)}), f32[768,1536]{1,0:T(8,128)}) %all-gather.12.cloned.1.call-update) | async-done | bytes 4718608 | tf_op jit(solution)/shard_map/all_gather | solution.py:342
  1622.6 142.8 %all-gather.10.cloned.1.call-done = f32[384,6400]{1,0:T(8,128)} async-done(((f32[48,6400]{1,0:T(8,128)}), f32[384,6400]{1,0:T(8,128)}) %all-gather.10.cloned.1.call-update) | async-done | bytes 9830416 | tf_op jit(solution)/shard_map/all_gather | solution.py:336
  (703 shorter events, 496.1 us)
Async XLA Ops:
  7.2 56.6 %collective-permute-start = (bf16[384,6400]{1,0:T(8,128)(2,1)}, bf16[384,6400]{1,0:T(8,128)(2,1)S(1)}, u32[]{:S(2)}, u32[]{:S(2)}) collective-permute-start(bf16[384,6400]{1,0:T(8,128)(2,1)} %param.17), channel_id=1, source_target_pairs={{0,3},{1,0},{2,1},{3,2},{4,7},{5,4},{6,5},{7,6},{8,11},{9,8},{10,9... | collective-permute-start | bytes 14745608 | tf_op jit(solution)/shard_map/ppermute | solution.py:17
  66.0 55.5 %collective-permute-start.1 = (bf16[384,6400]{1,0:T(8,128)(2,1)S(1)}, bf16[384,6400]{1,0:T(8,128)(2,1)}, u32[]{:S(2)}, u32[]{:S(2)}) collective-permute-start(bf16[384,6400]{1,0:T(8,128)(2,1)S(1)} %collective-permute-done), channel_id=1, source_target_pairs={{0,3},{1,0},{2,1},{3,2},{4,7},{5,4},{6,5},{7,6},{8,11},{9,8},{10,9... | collective-permute-start | bytes 14745608 | tf_op jit(solution)/shard_map/ppermute | solution.py:17
  121.5 87.5 %collective-permute-start.2 = (bf16[384,6400]{1,0:T(8,128)(2,1)}, bf16[384,6400]{1,0:T(8,128)(2,1)}, u32[]{:S(2)}, u32[]{:S(2)}) collective-permute-start(bf16[384,6400]{1,0:T(8,128)(2,1)} %collective-permute-done.1), channel_id=1, source_target_pairs={{0,3},{1,0},{2,1},{3,2},{4,7},{5,4},{6,5},{7,6},{8,11},{9,8},{10,9... | collective-permute-start | bytes 14745608 | tf_op jit(solution)/shard_map/ppermute | solution.py:17
  188.9 55.2 %all-to-all-start = ((bf16[128,8,6]{0,2,1:T(8,128)(2,1)}), bf16[128,8,6]{0,2,1:T(8,128)(2,1)S(1)}, u32[]{:S(2)}, u32[]{:S(2)}) async-start(bf16[128,8,6]{0,2,1:T(8,128)(2,1)} %all_to_all.106), calls=%async_computation | async-start | bytes 32768 | tf_op jit(solution)/shard_map/all_to_all | solution.py:184
  194.7 227.4 %all-gather.8.cloned.1.call-start = ((), (), s32[]{:S(2)}) async-start(), calls=%async_computation.13 | async-start | bytes 11796480 | tf_op jit(solution)/shard_map/all_gather | solution.py:146
  244.9 20.5 %all-to-all-start.2 = ((bf16[128,8,256]{2,0,1:T(8,128)(2,1)}), bf16[128,8,256]{2,0,1:T(8,128)(2,1)S(1)}, u32[]{:S(2)}, u32[]{:S(2)}) async-start(bf16[128,8,256]{2,0,1:T(8,128)(2,1)} %tile.28), calls=%async_computation.2 | async-start | bytes 1048576 | tf_op jit(solution)/shard_map/all_to_all | solution.py:185
  265.4 24.0 %all-to-all-start.1 = ((bf16[128,8,384]{2,0,1:T(8,128)(2,1)}), bf16[128,8,384]{2,0,1:T(8,128)(2,1)S(1)}, u32[]{:S(2)}, u32[]{:S(2)}) async-start(bf16[128,8,384]{2,0,1:T(8,128)(2,1)} %bitcast.416), calls=%async_computation.1 | async-start | bytes 1572864 | tf_op jit(solution)/shard_map/all_to_all | solution.py:177
  284.7 154.0 %copy-start.73 = (f32[48]{0:T(128)}, f32[48]{0:T(128)S(1)}, u32[]{:S(2)}) copy-start(f32[48]{0:T(128)S(1)} %convert_element_type.138) | copy-start | bytes 580
  289.5 98.6 %all-to-all-start.3 = ((bf16[128,8,384]{0,2,1:T(8,128)(2,1)}), bf16[128,8,384]{0,2,1:T(8,128)(2,1)}, u32[]{:S(2)}, u32[]{:S(2)}) async-start(bf16[128,8,384]{0,2,1:T(8,128)(2,1)} %bitcast.18), calls=%async_computation.3 | async-start | bytes 1572864 | tf_op jit(solution)/shard_map/all_to_all | solution.py:176
  396.3 25.2 %all-to-all-start.4 = ((bf16[8,128,384]{2,1,0:T(8,128)(2,1)}), bf16[8,128,384]{2,1,0:T(8,128)(2,1)S(1)}, u32[]{:S(2)}, u32[]{:S(2)}) async-start(bf16[8,128,384]{2,1,0:T(8,128)(2,1)} %bitcast.582), calls=%async_computation.4 | async-start | bytes 1572864 | tf_op jit(solution)/shard_map/all_to_all | solution.py:217
  434.4 23.9 %all-to-all-start.5 = ((bf16[128,8,384]{0,2,1:T(8,128)(2,1)}), bf16[128,8,384]{0,2,1:T(8,128)(2,1)}, u32[]{:S(2)}, u32[]{:S(2)}) async-start(bf16[128,8,384]{0,2,1:T(8,128)(2,1)} %bitcast.585), calls=%async_computation.5 | async-start | bytes 1572864 | tf_op jit(solution)/shard_map/all_to_all | solution.py:230
  438.6 298.2 %reduce-scatter.8.cloned.1.call-start = ((), (), s32[]{:S(2)}) async-start(), calls=%async_computation.14 | async-start | bytes 589824 | tf_op jit(solution)/shard_map/reduce_scatter | solution.py:255
  663.8 277.7 %reduce-scatter.12.cloned.1.call-start = ((), (), s32[]{:S(2)}) async-start(), calls=%async_computation.17 | async-start | bytes 19464192 | tf_op jit(solution)/shard_map/reduce_scatter | solution.py:328
  675.8 10.1 all-to-all-start.8
  710.2 25.4 %all-to-all-start.6 = ((bf16[8,128,384]{2,1,0:T(8,128)(2,1)}), bf16[8,128,384]{2,1,0:T(8,128)(2,1)S(1)}, u32[]{:S(2)}, u32[]{:S(2)}) async-start(bf16[8,128,384]{2,1,0:T(8,128)(2,1)} %bitcast.29), calls=%async_computation.6 | async-start | bytes 1572864 | tf_op jit(solution)/shard_map/all_to_all | solution.py:241
  713.8 591.9 %reduce-scatter.10.cloned.1.call-start = ((), (), s32[]{:S(2)}) async-start(), calls=%async_computation.15 | async-start | bytes 40550400 | tf_op jit(solution)/shard_map/reduce_scatter | solution.py:285
  803.2 634.9 %all-reduce.33.cloned.1.call-start = ((), (), s32[]{:S(2)}) async-start(), calls=%async_computation.20 | async-start | bytes 192512
  811.0 730.0 %reduce-scatter.14.cloned.1.call-start = ((), (), s32[]{:S(2)}) async-start(), calls=%async_computation.19 | async-start | bytes 811008 | tf_op jit(solution)/shard_map/reduce_scatter | solution.py:291
  812.3 493.4 %copy-start.81 = (u32[32]{0:T(128)S(1)}, u32[32]{0:T(128)}, u32[]{:S(2)}) copy-start(u32[32]{0:T(128)} %constant.221) | copy-start | bytes 388
  812.3 496.0 %copy-start.28 = (bf16[1,128,1536]{2,1,0:T(8,128)(2,1)S(1)}, bf16[1,128,1536]{2,1,0:T(8,128)(2,1)}, u32[]{:S(2)}) copy-start(bf16[1,128,1536]{2,1,0:T(8,128)(2,1)} %param.16) | copy-start | bytes 1179652
  812.3 496.0 %copy-start.37 = (f32[4,1,768]{2,1,0:T(1,128)S(1)}, f32[4,1,768]{2,1,0:T(1,128)}, u32[]{:S(2)}) copy-start(f32[4,1,768]{2,1,0:T(1,128)} %copy-done.36) | copy-start | bytes 36868
  812.3 496.0 %copy-start.67 = (f32[128]{0:T(128)S(1)}, f32[128]{0:T(128)}, u32[]{:S(2)}) copy-start(f32[128]{0:T(128)} %copy-done.66) | copy-start | bytes 1540
  812.3 810.3 %all-gather.12.cloned.1.call-start = ((), (), s32[]{:S(2)}) async-start(), calls=%async_computation.18 | async-start | bytes 5308416 | tf_op jit(solution)/shard_map/all_gather | solution.py:342
  941.5 823.9 %all-gather.10.cloned.1.call-start = ((), (), s32[]{:S(2)}) async-start(), calls=%async_computation.16 | async-start | bytes 11059200 | tf_op jit(solution)/shard_map/all_gather | solution.py:336
  (106 other events, 929.4 us)
Sparse Core Ops, SparseCore 0:
  197.1 65.5 all-gather.7
  663.9 62.6 reduce-scatter.7
  733.0 208.4 reduce-scatter.11
  947.8 357.8 reduce-scatter.9
  1313.1 124.8 all-reduce.32
  1443.6 97.3 reduce-scatter.13
  1543.2 79.3 all-gather.11
  1624.8 140.5 all-gather.9
